TPU v7x, 32 devices: a whole 2x2x4 slice. The times are simulated.
32 devices in a mesh: ctx: 8 (over y, x, core), exp: 4 (over z).
Axes of the slice: x: 2, y: 2, z: 4, core: 2. Of those that a mesh axis runs over, the one named last changes fastest.
Arguments:
- hidden_in: bfloat16 [1024, 4096], P('ctx', 'exp'), may hold values from -6 to 6
- query_vectors: bfloat16 [1024, 2048], P('ctx', 'exp'), may hold values from -6 to 6
- key_vectors: bfloat16 [1024, 2048], P('ctx', 'exp'), may hold values from -6 to 6
- value_vectors: bfloat16 [1024, 2048], P('ctx', 'exp'), may hold values from -24 to 24
- out_weight: bfloat16 [2048, 4096], P('exp'), may hold values from -0.125 to 0.125
- norm_gain: float32 [4096], replicated, may hold values from 0.5 to 1.5
- gate_proj: bfloat16 [4, 4096, 11008], P('exp', None, 'ctx'), may hold values from -0.09375 to 0.09375
- up_proj: bfloat16 [4, 4096, 11008], P('exp', None, 'ctx'), may hold values from -0.09375 to 0.09375
- down_proj: bfloat16 [4, 11008, 4096], P('exp', 'ctx'), may hold values from -0.0546875 to 0.0546875
- expert_ids: int32 [1024, 2], P('ctx'), may hold values from 0 to 3, all different within a row; in each aligned block of 128 rows (0 to 127, 128 to 255, ...) at most 80 rows name the same one
- gate_scale: float32 [1024, 2], P('ctx'), may hold values from 0.1 to 1
Outputs:
- layer_out: bfloat16 [1024, 4096], P('ctx', 'exp')
Inputs may be any that keep to these rules, and one draw needn't show every extreme that they name: `expert_ids`: each row names two different experts. In each aligned block of 128 rows (the rows of one ctx device) no expert is named by more than 80 rows, and in some blocks some expert is named by exactly 80 rows.
All inputs are finite; a program needn't handle non-finite values.
Results may differ from a plain program's by a relative error of at most 0.017.
Values may be sent and summed in bfloat16 or wider, within the bound.
A program may use at most 128 MiB of HBM per device.

v0:
```python
import functools

import jax
import jax.numpy as jnp
from jax import lax
from jax.experimental import pallas as pl
from jax.experimental.pallas import tpu as pltpu
from jax.sharding import PartitionSpec as P

HEAD_DIM = 128
MESH = pl.DeviceIdType.MESH

epsilon = 1e-05
masked_score = -1e30
PIECES = 4


def mixed(index, flip):
    result = index
    bit = 1
    while bit <= flip:
        if flip & bit:
            result = result + bit - 2 * bit * ((index // bit) % 2)
        bit *= 2
    return result


def remote(src, dst, send_sem, recv_sem, device):
    return pltpu.make_async_remote_copy(
        src_ref=src, dst_ref=dst, send_sem=send_sem, recv_sem=recv_sem,
        device_id=device, device_id_type=MESH,
    )


def greet(devices):
    barrier = pltpu.get_barrier_semaphore()
    for device in devices:
        pl.semaphore_signal(barrier, inc=1, device_id=device, device_id_type=MESH)
    pl.semaphore_wait(barrier, len(devices))


def gather_kernel(chips, k_ref, v_ref, ko_ref, vo_ref, local_sem, send_sem, pass_sem, recv_sem, half_send, half_recv):
    ctx, exp = lax.axis_index("ctx"), lax.axis_index("exp")
    chip, core = ctx // 2, ctx % 2
    rows = k_ref.shape[0]
    partner = (chip * 2 + 1 - core, exp)
    others = [(((chip + j) % chips) * 2 + core, exp) for j in range(1, chips)]
    pairs = ((k_ref, ko_ref), (v_ref, vo_ref))
    width = k_ref.shape[1]
    square = chips == 4
    near = (1, 2) if square else tuple(range(chips - 1, 0, -1))

    def device_of(j):
        return (mixed(chip, j) * 2 + core, exp) if square else others[j - 1]

    def source_of(j):
        return mixed(chip, j) if square else (chip + chips - j) % chips

    def half(ref, owner, which):
        part = pl.ds(pl.multiple_of(owner * rows, rows), rows)
        return ref.at[part, pl.ds(which * (width // 2), width // 2)]

    def block(ref, owner):
        return ref.at[pl.ds(pl.multiple_of(owner * rows, rows), rows), :]

    own = []
    for i, (src, dst) in enumerate(pairs):
        own.append(pltpu.make_async_copy(src, block(dst, ctx), local_sem.at[i]))
        own[-1].start()
    greet([partner] + others)
    sent = []
    for i, (src, dst) in enumerate(pairs):
        for j in near:
            sent.append(remote(src, block(dst, ctx), send_sem.at[i, j], recv_sem.at[i, ctx], device_of(j)))
            sent[-1].start()
        sent.append(remote(src, block(dst, ctx), send_sem.at[i, 0], recv_sem.at[i, ctx], partner))
        sent[-1].start()
    for i, (src, dst) in enumerate(pairs):
        for j in near:
            owner = source_of(j) * 2 + core
            here = block(dst, owner)
            passed = remote(here, here, pass_sem.at[i, j], recv_sem.at[i, owner], partner)
            passed.wait_recv()
            if square:
                piece = half(dst, owner, j - 1)
                sent.append(remote(piece, piece, half_send.at[i, j - 1], half_recv.at[i, j - 1], device_of(3 - j)))
                sent[-1].start()
            passed.start()
            sent.append(passed)
    for i, (src, dst) in enumerate(pairs):
        if square:
            owner = mixed(chip, 3) * 2 + core
            for h in range(2):
                piece = half(dst, owner, h)
                remote(piece, piece, half_send.at[i, h], half_recv.at[i, h], partner).wait_recv()
            here = block(dst, owner)
            sent.append(remote(here, here, pass_sem.at[i, 3], recv_sem.at[i, owner], partner))
            sent[-1].start()
    for i, (src, dst) in enumerate(pairs):
        for j in range(chips):
            owner = ((chip + chips - j) % chips) * 2 + 1 - core
            here = block(dst, owner)
            remote(here, here, pass_sem.at[i, 0], recv_sem.at[i, owner], partner).wait_recv()
    for copy in sent:
        copy.wait_send()
    for copy in own:
        copy.wait()


def gather_blocks(chips, keys, values):
    rows, width = keys.shape
    whole = jax.ShapeDtypeStruct((rows * chips * 2, width), keys.dtype)
    return pl.pallas_call(
        functools.partial(gather_kernel, chips),
        out_shape=(whole, whole),
        in_specs=[pl.BlockSpec(memory_space=pltpu.VMEM)] * 2,
        out_specs=[pl.BlockSpec(memory_space=pltpu.VMEM)] * 2,
        scratch_shapes=[
            pltpu.SemaphoreType.DMA((2,)),
            pltpu.SemaphoreType.DMA((2, chips)),
            pltpu.SemaphoreType.DMA((2, chips)),
            pltpu.SemaphoreType.DMA((2, chips * 2)),
            pltpu.SemaphoreType.DMA((2, 2)),
            pltpu.SemaphoreType.DMA((2, 2)),
        ],
        compiler_params=pltpu.CompilerParams(collective_id=0, has_side_effects=True),
        name="gather_blocks",
    )(keys, values)


def project_kernel(experts, att_ref, weight_ref, hidden_ref, out_ref, terms, landed, send_sem, recv_sem):
    ctx, exp = lax.axis_index("ctx"), lax.axis_index("exp")
    width = hidden_ref.shape[1]
    levels = experts.bit_length() - 1
    depth = hidden_ref.shape[0] // PIECES
    peers = [(ctx, mixed(exp, 1 << b)) for b in range(levels)]
    greet(peers)
    sent = []

    def slot(level, k):
        return sum(experts >> (b + 1) for b in range(level)) + k // (2 << level)

    def send(level, k, piece):
        to = slot(level, k - (1 << level))
        here = pl.ds(piece * depth, depth)
        sent.append(remote(
            terms.at[k, here], landed.at[to, here], send_sem.at[to, piece], recv_sem.at[to, piece], peers[level]
        ))
        sent[-1].start()

    order = [k for k in range(experts - 1, -1, -1) if k % 2] + [k for k in range(experts - 1, -1, -1) if not k % 2]
    for k in order:
        columns = pl.ds(pl.multiple_of(mixed(exp, k) * width, width), width)
        terms[k] = jnp.dot(
            att_ref[...], weight_ref[:, columns], preferred_element_type=jnp.float32
        ).astype(jnp.bfloat16)
        if k % 2:
            for piece in range(PIECES):
                send(0, k, piece)
    for level in range(levels):
        for k in range(experts - (2 << level), -1, -(2 << level)):
            at = slot(level, k)
            for piece in range(PIECES):
                here = pl.ds(piece * depth, depth)
                view = landed.at[at, here]
                remote(view, view, send_sem.at[at, piece], recv_sem.at[at, piece], peers[level]).wait_recv()
                total = terms[k, here, :].astype(jnp.float32) + landed[at, here, :].astype(jnp.float32)
                if level + 1 < levels:
                    terms[k, here, :] = total.astype(jnp.bfloat16)
                    if k & (2 << level):
                        send(level + 1, k, piece)
                else:
                    out_ref[here, :] = (hidden_ref[here, :].astype(jnp.float32) + total).astype(jnp.bfloat16)
    for copy in sent:
        copy.wait_send()


def project(experts, attended, weight, hidden):
    rows, width = hidden.shape
    return pl.pallas_call(
        functools.partial(project_kernel, experts),
        out_shape=jax.ShapeDtypeStruct((rows, width), jnp.bfloat16),
        in_specs=[pl.BlockSpec(memory_space=pltpu.VMEM)] * 3,
        out_specs=pl.BlockSpec(memory_space=pltpu.VMEM),
        scratch_shapes=[
            pltpu.VMEM((experts, rows, width), jnp.bfloat16),
            pltpu.VMEM((experts - 1, rows, width), jnp.bfloat16),
            pltpu.SemaphoreType.DMA((experts - 1, PIECES)),
            pltpu.SemaphoreType.DMA((experts - 1, PIECES)),
        ],
        compiler_params=pltpu.CompilerParams(
            collective_id=1, has_side_effects=True, vmem_limit_bytes=32 * 1024 * 1024
        ),
        name="project_reduce",
    )(attended, weight, hidden)


def tiles(width, body, size=256):
    full = width // size
    if full:
        @pl.loop(0, full)
        def _(t):
            body(pl.ds(pl.multiple_of(t * size, size), size))
    if width % size:
        body(pl.ds(full * size, width % size))


def times_transposed(left, right):
    return lax.dot_general(
        left, right, (((1,), (1,)), ((), ())), preferred_element_type=jnp.float32
    )


def experts_kernel(
    chips, experts, buf, gain, gate_hbm, up_hbm, down_hbm, out,
    rows_all, wg, wu, wd, acc_g, acc_u, scaled, hidden, squares, pair_in, chip_in, final,
    w_sem, local_sem, a2a_send, ag_send, pass_send, ag_recv,
    pair_send, pair_recv, rs_send, rs_recv, ret_send, ret_recv,
):
    ctx, exp = lax.axis_index("ctx"), lax.axis_index("exp")
    chip, core = ctx // 2, ctx % 2
    cap, width = buf.shape[1:]
    total_rows = chips * 2 * cap
    features = gate_hbm.shape[2]
    inner = gate_hbm.shape[1]
    partner = (chip * 2 + 1 - core, exp)
    others = [(((chip + j) % chips) * 2 + core, exp) for j in range(1, chips)]
    peers = [(ctx, mixed(exp, k)) for k in range(1, experts)]

    loads = []
    for k in range(experts):
        part = pl.ds(pl.multiple_of(mixed(exp, k) * width, width), width)
        loads.append((
            pltpu.make_async_copy(gate_hbm.at[0, :, part], wg.at[k], w_sem.at[0, k]),
            pltpu.make_async_copy(up_hbm.at[0, :, part], wu.at[k], w_sem.at[1, k]),
        ))
    downs = []
    for k in range(experts):
        part = pl.ds(pl.multiple_of(mixed(exp, k) * width, width), width)
        downs.append(pltpu.make_async_copy(down_hbm.at[0, :, part], wd.at[k], w_sem.at[2, k]))

    def span(index):
        return pl.ds(pl.multiple_of(index * cap, cap), cap)

    mine = core * chips + chip

    own = pltpu.make_async_copy(buf.at[0], rows_all.at[0, span(mine), :], local_sem.at[0])
    own.start()
    for gate_load, up_load in loads:
        gate_load.start()
        up_load.start()
    for k in range(experts - 1, -1, -1):
        downs[k].start()
    greet([partner] + others + peers)

    sent = []
    for k in range(1, experts):
        copy = remote(buf.at[k], rows_all.at[k, span(mine), :], a2a_send.at[k], ag_recv.at[k, mine], peers[k - 1])
        copy.start()
        sent.append(copy)

    def spread(k):
        here = rows_all.at[k, span(mine), :]
        if k == 0:
            own.wait()
        else:
            remote(here, here, a2a_send.at[k], ag_recv.at[k, mine], partner).wait_recv()
        for j in range(chips - 1, 0, -1):
            copy = remote(here, here, ag_send.at[k, j], ag_recv.at[k, mine], others[j - 1])
            copy.start()
            sent.append(copy)
        copy = remote(here, here, ag_send.at[k, 0], ag_recv.at[k, mine], partner)
        copy.start()
        sent.append(copy)

    def collect(k):
        for j in range(1, chips):
            owner = core * chips + (chip + chips - j) % chips
            here = rows_all.at[k, span(owner), :]
            copy = remote(here, here, pass_send.at[k, j], ag_recv.at[k, owner], partner)
            copy.wait_recv()
            copy.start()
            sent.append(copy)
        for j in range(chips):
            owner = (1 - core) * chips + (chip + chips - j) % chips
            here = rows_all.at[k, span(owner), :]
            remote(here, here, pass_send.at[k, 0], ag_recv.at[k, owner], partner).wait_recv()

    spread(0)
    spread(1)
    for k in range(experts):
        collect(k)
        if k + 2 < experts:
            spread(k + 2)
        gain_row = gain[mixed(exp, k)]

        @pl.loop(0, chips * 2)
        def _(b, k=k, gain_row=gain_row):
            x = rows_all[k, span(b), :].astype(jnp.float32)
            square = jnp.broadcast_to(jnp.sum(x * x, axis=1, keepdims=True), (cap, 128))
            squares[span(b), :] = square if k == 0 else squares[span(b), :] + square
            scaled[span(b), :] = (x * gain_row).astype(jnp.bfloat16)

        loads[k][0].wait()
        loads[k][1].wait()
        last = k == experts - 1
        if last:
            squares[...] = lax.rsqrt(squares[...] * (1.0 / features) + epsilon)

        def up_tile(cols, k=k, last=last):
            g = times_transposed(scaled[...], wg[k, cols, :])
            u = times_transposed(scaled[...], wu[k, cols, :])
            if k:
                g = g + acc_g[:, cols]
                u = u + acc_u[:, cols]
            if last:
                inverse = squares[:, 0:1]
                g = g * inverse
                u = u * inverse
                hidden[:, cols] = (g / (1.0 + jnp.exp(-g)) * u).astype(jnp.bfloat16)
            else:
                acc_g[:, cols] = g
                acc_u[:, cols] = u

        tiles(inner, up_tile)

    for copy in sent:
        copy.wait_send()
    sent = []
    half = chips * cap

    def half_of(which):
        return pl.ds(pl.multiple_of(which * half, half), half)

    def multiply(k):
        downs[k].wait()

        def down_tile(cols):
            rows_all[k, :, cols] = jnp.dot(
                hidden[...], wd[k, :, cols], preferred_element_type=jnp.float32
            ).astype(jnp.bfloat16)

        tiles(width, down_tile)
        copy = remote(rows_all.at[k, half_of(1 - core), :], pair_in.at[k], pair_send.at[k], pair_recv.at[k], partner)
        copy.start()
        sent.append(copy)

    def merge(k):
        remote(pair_in.at[k], pair_in.at[k], pair_send.at[k], pair_recv.at[k], partner).wait_recv()
        for j in range(chips - 1, -1, -1):
            to = (chip + j) % chips
            place = span(core * chips + to)
            rows_all[k, place, :] = (
                rows_all[k, place, :].astype(jnp.float32) + pair_in[k, span(to), :].astype(jnp.float32)
            ).astype(jnp.bfloat16)
            if j:
                copy = remote(rows_all.at[k, place, :], chip_in.at[k, j - 1], rs_send.at[k, j], rs_recv.at[k, j], others[j - 1])
                copy.start()
                sent.append(copy)

    def finish(k):
        value = rows_all[k, span(mine), :].astype(jnp.float32)
        for j in range(1, chips):
            here = chip_in.at[k, j - 1]
            remote(here, here, rs_send.at[k, j], rs_recv.at[k, j], partner).wait_recv()
            value = value + chip_in[k, j - 1].astype(jnp.float32)
        if k == 0:
            out[0] = value.astype(jnp.bfloat16)
        else:
            final[k] = value.astype(jnp.bfloat16)
            copy = remote(final.at[k], out.at[k], ret_send.at[k], ret_recv.at[k], peers[k - 1])
            copy.start()
            sent.append(copy)

    order = list(range(experts - 1, -1, -1))
    for step in range(experts + 2):
        if step < experts:
            multiply(order[step])
        if 1 <= step <= experts:
            merge(order[step - 1])
        if step >= 2:
            finish(order[step - 2])
    for k in range(1, experts):
        remote(out.at[k], out.at[k], ret_send.at[k], ret_recv.at[k], peers[k - 1]).wait_recv()
    for copy in sent:
        copy.wait_send()


def run_experts(chips, experts, buffer, gain, gate, up, down):
    _, cap, width = buffer.shape
    inner = gate.shape[1]
    rows = chips * 2 * cap
    bf16, f32 = jnp.bfloat16, jnp.float32
    dma = pltpu.SemaphoreType.DMA
    vmem = pl.BlockSpec(memory_space=pltpu.VMEM)
    hbm = pl.BlockSpec(memory_space=pl.ANY)
    return pl.pallas_call(
        functools.partial(experts_kernel, chips, experts),
        out_shape=jax.ShapeDtypeStruct((experts, cap, width), bf16),
        in_specs=[vmem, vmem, hbm, hbm, hbm],
        out_specs=vmem,
        scratch_shapes=[
            pltpu.VMEM((experts, rows, width), bf16),
            pltpu.VMEM((experts, inner, width), bf16),
            pltpu.VMEM((experts, inner, width), bf16),
            pltpu.VMEM((experts, inner, width), bf16),
            pltpu.VMEM((rows, inner), f32),
            pltpu.VMEM((rows, inner), f32),
            pltpu.VMEM((rows, width), bf16),
            pltpu.VMEM((rows, inner), bf16),
            pltpu.VMEM((rows, 128), f32),
            pltpu.VMEM((experts, chips * cap, width), bf16),
            pltpu.VMEM((experts, chips - 1, cap, width), bf16),
            pltpu.VMEM((experts, cap, width), bf16),
            dma((3, experts)),
            dma((1,)),
            dma((experts,)),
            dma((experts, chips)),
            dma((experts, chips)),
            dma((experts, chips * 2)),
            dma((experts,)),
            dma((experts,)),
            dma((experts, chips)),
            dma((experts, chips)),
            dma((experts,)),
            dma((experts,)),
        ],
        compiler_params=pltpu.CompilerParams(
            collective_id=2, has_side_effects=True, vmem_limit_bytes=67043328
        ),
        name="experts",
    )(buffer, gain, gate, up, down)


def attend(query_heads, key_rows, value_rows, query_offset):
    head_count, row_count, head_width = query_heads.shape
    key_count = key_rows.shape[0]
    key_split = key_rows.reshape(key_count, head_count, head_width)
    value_split = value_rows.reshape(key_count, head_count, head_width)
    scores = jnp.einsum(
        "hqd,khd->hqk", query_heads, key_split, preferred_element_type=jnp.float32
    ) * HEAD_DIM ** (-0.5)
    query_pos = query_offset + lax.broadcasted_iota(jnp.int32, (row_count, key_count), 0)
    key_pos = lax.broadcasted_iota(jnp.int32, (row_count, key_count), 1)
    visible = key_pos <= query_pos
    scores = jnp.where(visible[None], scores, masked_score)
    top = jnp.max(scores, axis=2)
    weights = jnp.where(visible[None], jnp.exp(scores - top[..., None]), 0.0)
    weighted = jnp.einsum(
        "hqk,khd->hqd",
        weights.astype(jnp.bfloat16),
        value_split,
        preferred_element_type=jnp.float32,
    )
    return weighted / jnp.sum(weights, axis=2)[..., None]


def local(
    hidden_in,
    query_vectors,
    key_vectors,
    value_vectors,
    out_weight,
    norm_gain,
    gate_proj,
    up_proj,
    down_proj,
    expert_ids,
    gate_scale,
):
    row_count, local_width = hidden_in.shape
    head_count = query_vectors.shape[1] // HEAD_DIM
    chips = lax.axis_size("ctx") // 2
    expert_count = lax.axis_size("exp")
    query_heads = query_vectors.reshape(row_count, head_count, HEAD_DIM).transpose(1, 0, 2)
    keys, values = gather_blocks(chips, key_vectors, value_vectors)
    attended = (
        attend(query_heads, keys, values, lax.axis_index("ctx") * row_count)
        .transpose(1, 0, 2)
        .reshape(row_count, head_count * HEAD_DIM)
        .astype(jnp.bfloat16)
    )
    capacity = min(row_count, 5 * row_count // (2 * expert_count))
    capacity = -(-capacity // 16) * 16
    flat_ids = jnp.bitwise_xor(expert_ids.reshape(row_count * 2), lax.axis_index("exp"))
    onehot = (
        flat_ids[:, None] == lax.broadcasted_iota(jnp.int32, (row_count * 2, expert_count), 1)
    ).astype(jnp.int32)
    earlier = jnp.cumsum(onehot, axis=0) - onehot
    slot_index = jnp.sum(earlier * onehot, axis=1)
    target = flat_ids * capacity + slot_index
    placing = (
        target[None, :]
        == lax.broadcasted_iota(jnp.int32, (expert_count * capacity, row_count * 2), 0)
    ).astype(jnp.bfloat16)
    placing_tokens = jnp.sum(placing.reshape(expert_count * capacity, row_count, 2), axis=2)
    residual = project(expert_count, attended, out_weight, hidden_in)
    buffer = jnp.dot(placing_tokens, residual, preferred_element_type=jnp.float32).astype(
        jnp.bfloat16
    )
    returned = run_experts(
        chips,
        expert_count,
        buffer.reshape(expert_count, capacity, local_width),
        norm_gain.reshape(expert_count, 1, local_width),
        gate_proj.transpose(0, 2, 1),
        up_proj.transpose(0, 2, 1),
        down_proj,
    ).reshape(expert_count * capacity, local_width)
    gathered_back = lax.dot_general(
        placing, returned, (((0,), (0,)), ((), ())), preferred_element_type=jnp.float32
    )
    gathered_back = gathered_back.reshape(row_count, 2, local_width)
    combined = (
        residual.astype(jnp.float32)
        + gate_scale[:, 0:1] * gathered_back[:, 0]
        + gate_scale[:, 1:2] * gathered_back[:, 1]
    )
    return combined.astype(jnp.bfloat16)


def solution(mesh):
    placed = (
        P("ctx", "exp"),
        P("ctx", "exp"),
        P("ctx", "exp"),
        P("ctx", "exp"),
        P("exp", None),
        P(),
        P("exp", None, "ctx"),
        P("exp", None, "ctx"),
        P("exp", "ctx", None),
        P("ctx", None),
        P("ctx", None),
    )
    return jax.shard_map(
        local, mesh=mesh, in_specs=placed, out_specs=P("ctx", "exp"), check_vma=False
    )
```

profile of v0, /device:TPU:0, one launch (start us, length us, event | category | flops | bytes accessed | tf_op | source)
XLA Modules:
  0.0 144.4 jit_solution(10353722963229582441)
XLA Ops:
  0.0 0.8 copy.34
  0.8 0.1 xor.26
  1.0 1.2 reduce-window.6
  2.2 0.1 slice.24
  2.3 0.1 copy.35
  2.4 0.1 copy.36
  2.5 0.1 add_bitcast_fusion
  2.6 0.1 xor.25
  2.8 0.1 reduce_sum.34
  2.9 0.1 copy.37
  3.0 0.1 fusion.20
  3.1 0.5 copy-done.5
  3.6 19.2 %gather_blocks.1 = (bf16[1024,512]{1,0:T(8,128)(2,1)}, bf16[1024,512]{1,0:T(8,128)(2,1)}) custom-call(bf16[128,512]{1,0:T(8,128)(2,1)} %k_ref.1, bf16[128,512]{1,0:T(8,128)(2,1)} %v_ref.1), custom_call_target="tpu_custom_call" | custom-call | tf_op jit(solution)/shard_map/gather_blocks/pallas_call | solution.py:113
  22.8 0.0 copy-start.3
  22.8 2.4 %copy.40 = bf16[1024,512]{0,1:T(8,128)(2,1)} copy(bf16[1024,512]{1,0:T(8,128)(2,1)} %get-tuple-element.8) | data formatting | bytes 2097152 | tf_op jit(solution)/shard_map/reshape | solution.py:439
  25.2 0.0 copy-done.4
  25.2 0.4 fusion.4
  25.6 0.1 iota_compare_fusion
  25.7 1.0 fusion.38
  26.8 2.3 %fusion.3 = bf16[128,4,128]{0,2,1:T(8,128)(2,1)S(1)} fusion(bf16[1024,4,128]{0,2,1:T(8,128)(2,1)} %bitcast.120, f32[4,1024,128]{2,1,0:T(8,128)S(1)} %fusion.4, pred[128,1024]{0,1:T(8,128)(4,1)S(1)} %iota_compare_fusion, f32[128,4]{0,1:T(4,128)S(1)} %bitcast.124), kind=kOutput, calls=%fused_computation.7 | convolution fusion | flops 136971776 | bytes 3409920 | tf_op jit(solution)/shard_map/hqk,khd->hqd/dot_general | solution.py:449
  29.1 0.1 copy.41.att_ref
  29.2 0.0 copy-done.2
  29.2 0.0 copy-start
  29.2 2.2 %copy-done = bf16[512,4096]{1,0:T(8,128)(2,1)S(1)} copy-done((bf16[512,4096]{1,0:T(8,128)(2,1)S(1)}, bf16[512,4096]{1,0:T(8,128)(2,1)}, u32[]{:S(2)}) %copy-start) | copy-done | bytes 4194328
  31.4 22.7 %project_reduce.1 = bf16[128,1024]{1,0:T(8,128)(2,1)S(1)} custom-call(bf16[128,512]{1,0:T(8,128)(2,1)S(1)} %copy.41.att_ref, bf16[512,4096]{1,0:T(8,128)(2,1)S(1)} %copy-done, bf16[128,1024]{1,0:T(8,128)(2,1)S(1)} %copy-done.2), custom_call_target="tpu_custom_call" | custom-call | tf_op jit(solution)/shard_map/project_reduce/pallas_call | solution.py:180
  54.1 0.0 copy-start.1
  54.1 0.7 copy-done.1
  54.8 1.2 convolution_convert_fusion
  56.0 84.3 %experts.1 = bf16[4,80,1024]{2,1,0:T(8,128)(2,1)} custom-call(bf16[4,80,1024]{2,1,0:T(8,128)(2,1)} %bitcast.119, f32[4,1,1024]{2,1,0:T(1,128)} %bitcast.122, bf16[1,1376,4096]{2,1,0:T(8,128)(2,1)} %bitcast.116, bf16[1,1376,4096]{2,1,0:T(8,128)(2,1)} %bitcast.117, bf16[1,1376,4096]{2,1,0:T(8,128)(2,1)} %down_hbm.1), custom_call_target="tpu_custom_call" | custom-call | tf_op jit(solution)/shard_map/experts/pallas_call | solution.py:397
  140.2 1.6 %fusion.17 = f32[128,2,1024]{2,0,1:T(8,128)S(1)} fusion(bf16[320,1024,1]{1,0,2:T(8,128)(2,1)} %bitcast.118, s32[128,2]{0,1:T(2,128)} %copy-done.5), kind=kOutput, calls=%fused_computation.26 | convolution fusion | flops 167854080 | bytes 1704960 | tf_op jit(solution)/shard_map/dot_general | solution.py:510
  141.8 0.8 slice_bitcast_fusion.3
  142.6 1.8 %fusion.13 = bf16[128,1024]{1,0:T(8,128)(2,1)} fusion(f32[128,2,1024]{2,0,1:T(8,128)S(1)} %fusion.17, bf16[128,1024]{1,0:T(8,128)(2,1)} %copy-done.1, f32[128]{0:T(128)S(1)} %get-tuple-element.10, f32[128]{0:T(128)S(1)} %get-tuple-element.9), kind=kLoop, calls=%fused_computation.18 | loop fusion | flops 786432 | bytes 1573888 | tf_op jit(solution)/shard_map/convert_element_type | solution.py:519
  (11 shorter events, 0.1 us)
Async XLA Ops:
  0.0 25.2 %copy-start.4 = (bf16[128,512]{1,0:T(8,128)(2,1)S(1)}, bf16[128,512]{1,0:T(8,128)(2,1)}, u32[]{:S(2)}) copy-start(bf16[128,512]{1,0:T(8,128)(2,1)} %param.12) | copy-start | bytes 393220
  3.0 0.6 copy-start.5
  22.8 2.4 %copy-start.3 = (bf16[1024,512]{1,0:T(8,128)(2,1)S(1)}, bf16[1024,512]{1,0:T(8,128)(2,1)}, u32[]{:S(2)}) copy-start(bf16[1024,512]{1,0:T(8,128)(2,1)} %get-tuple-element.7) | copy-start | bytes 3145732
  26.8 2.4 %copy-start.2 = (bf16[128,1024]{1,0:T(8,128)(2,1)S(1)}, bf16[128,1024]{1,0:T(8,128)(2,1)}, u32[]{:S(2)}) copy-start(bf16[128,1024]{1,0:T(8,128)(2,1)} %hidden_ref.1) | copy-start | bytes 786436
  29.2 2.2 %copy-start = (bf16[512,4096]{1,0:T(8,128)(2,1)S(1)}, bf16[512,4096]{1,0:T(8,128)(2,1)}, u32[]{:S(2)}) copy-start(bf16[512,4096]{1,0:T(8,128)(2,1)} %weight_ref.1) | copy-start | bytes 12582916
  54.1 0.7 copy-start.1
where the time goes:
time: 145 us; the launch traced here: 144 us
  Pallas kernels  126 us (87%)
  local copies, waits for them, and re-layouts  8.25 us (6%)
  matrix products  6.51 us (4%)
  other arithmetic  3.37 us (2%)
    pallas_call x1, Pallas kernels, run_experts(): pl.pallas_call(functools.partial(experts_kernel, chips, experts), out_sha...  84.3 us
    pallas_call x1, Pallas kernels, project(): pl.pallas_call(functools.partial(project_kernel, experts), out_shape=jax....  22.7 us
    pallas_call x1, Pallas kernels, gather_blocks(): pl.pallas_call(functools.partial(gather_kernel, chips), out_shape=(whole,...  19.2 us
    unnamed x13, local copies, waits for them, and re-layouts  4.24 us

commit v1 on v0

--- a/solution.py
+++ b/solution.py
@@ -432,6 +432,471 @@
     )(buffer, gain, gate, up, down)
 
 
+def eye_of(rows, columns):
+    return lax.broadcasted_iota(jnp.int32, (rows, columns), 0) == lax.broadcasted_iota(jnp.int32, (rows, columns), 1)
+
+
+def as_row(column, columns):
+    rows = column.shape[0]
+    return jnp.sum(jnp.where(eye_of(rows, columns), column, 0.0), axis=0, keepdims=True)
+
+
+def routed(ids_ref, scale_ref, onehot, weigh, cuts, experts, exp):
+    tokens = ids_ref.shape[1]
+    relative = lax.broadcasted_iota(jnp.int32, (experts, tokens), 0)
+    wanted = jnp.bitwise_xor(relative, exp)
+    first, second = ids_ref[0:1, :] == wanted, ids_ref[1:2, :] == wanted
+    member = (first | second).astype(jnp.float32)
+    gates = jnp.where(first, scale_ref[0:1, :], 0.0) + jnp.where(second, scale_ref[1:2, :], 0.0)
+    earlier = (
+        lax.broadcasted_iota(jnp.int32, (tokens, tokens), 0) < lax.broadcasted_iota(jnp.int32, (tokens, tokens), 1)
+    ).astype(jnp.bfloat16)
+    place = jnp.dot(member.astype(jnp.bfloat16), earlier, preferred_element_type=jnp.float32)
+    place = jnp.where(member > 0.5, place, -1.0).astype(jnp.int32)
+    base = 0
+    for r, count in enumerate(cuts):
+        slots = base + lax.broadcasted_iota(jnp.int32, (count, tokens), 0)
+        for k in range(experts):
+            chosen = slots == place[k:k + 1, :]
+            onehot[k, base:base + count, :] = chosen.astype(jnp.bfloat16)
+            gate = jnp.where(chosen, gates[k:k + 1, :], 0.0)
+            high = gate.astype(jnp.bfloat16)
+            rows = pl.ds(k * count, count)
+            weigh[r][0, rows, :] = high
+            weigh[r][1, rows, :] = (gate - high.astype(jnp.float32)).astype(jnp.bfloat16)
+        base += count
+
+
+def square_experts_kernel(
+    experts, cuts, residual, ids, scale, gain, gate_hbm, up_hbm, down_hbm, out,
+    onehot, weigh_a, weigh_b, normal, buf_a, buf_b, rows_a, rows_b, wg, wu, wd, acc_g, acc_u, part_g, part_u, hidden_a, hidden_b,
+    pair_a, pair_b, near_a, near_b, far_a, far_b, final_a, final_b, back_a, back_b, summed,
+    sums, sums_in, inverse_out, inverse_in, inverse_a, inverse_b,
+    w_sem, own_send, own_recv, near_send, near_recv, half_send, half_recv, pair_send, pair_recv,
+    swap_send, swap_recv, one_send, one_recv, two_send, two_recv, ret_send, ret_recv,
+    sum_send, sum_recv, inv_send, inv_recv,
+):
+    chips = 4
+    ctx, exp = lax.axis_index("ctx"), lax.axis_index("exp")
+    chip, core = ctx // 2, ctx % 2
+    tokens, width = residual.shape
+    features = gate_hbm.shape[2]
+    inner = gate_hbm.shape[1]
+    wing = width // 2
+    cap = sum(cuts)
+    weigh, buf, rows = (weigh_a, weigh_b), (buf_a, buf_b), (rows_a, rows_b)
+    hidden, pair_in, near_in, far_in = (hidden_a, hidden_b), (pair_a, pair_b), (near_a, near_b), (far_a, far_b)
+    final, back, inverse = (final_a, final_b), (back_a, back_b), (inverse_a, inverse_b)
+    partner = (chip * 2 + 1 - core, exp)
+    near = {j: (mixed(chip, j) * 2 + core, exp) for j in (1, 2)}
+    peers = [(ctx, mixed(exp, k)) for k in range(1, experts)]
+    plane = [(mixed(chip, j) * 2 + mixed(core, c), exp) for j in range(chips) for c in range(2)][1:]
+
+    def f32(value):
+        return value.astype(jnp.float32)
+
+    def chunk(k):
+        return pl.ds(k * width, width)
+
+    loads, downs = [], []
+    for k in range(experts):
+        part = pl.ds(pl.multiple_of(mixed(exp, k) * width, width), width)
+        loads.append((
+            pltpu.make_async_copy(gate_hbm.at[0, :, part], wg.at[:, chunk(k)], w_sem.at[0, k]),
+            pltpu.make_async_copy(up_hbm.at[0, :, part], wu.at[:, chunk(k)], w_sem.at[1, k]),
+        ))
+        downs.append(pltpu.make_async_copy(down_hbm.at[0, :, part], wd.at[k], w_sem.at[2, k]))
+    for gate_load, up_load in loads:
+        gate_load.start()
+        up_load.start()
+    for k in range(experts - 1, -1, -1):
+        downs[k].start()
+
+    def block(j, which):
+        return which * chips + mixed(chip, j)
+
+    def span(r, index):
+        return pl.ds(pl.multiple_of(index * cuts[r], cuts[r]), cuts[r])
+
+    def wings(k, way):
+        return pl.ds(k * width + (way - 1) * wing, wing)
+
+    mine = block(0, core)
+    started = {"sums": [], 0: [], 1: [], "back": []}
+
+    def begin(group, src, dst, send_sem, recv_sem, device):
+        copy = remote(src, dst, send_sem, recv_sem, device)
+        copy.start()
+        started[group].append(copy)
+
+    def arrive(view, recv_sem):
+        remote(view, view, sum_send.at[0], recv_sem, partner).wait_recv()
+
+    def settle(group):
+        for copy in started[group]:
+            copy.wait_send()
+        started[group].clear()
+
+    routed(ids, scale, onehot, weigh, cuts, experts, exp)
+    greet(plane + peers)
+
+    def prepare():
+        x = f32(residual[...])
+        normal[...] = (x * gain[exp]).astype(jnp.bfloat16)
+        total = as_row(jnp.sum(x * x, axis=1, keepdims=True), tokens)
+        sums[...] = jnp.broadcast_to(total, sums.shape)
+
+    def route(r, k):
+        base = sum(cuts[:r])
+        picked = jnp.dot(
+            onehot[k, base:base + cuts[r], :], normal[...], preferred_element_type=jnp.float32
+        ).astype(jnp.bfloat16)
+        if k == 0:
+            rows[r][span(r, mine), chunk(0)] = picked
+        else:
+            buf[r][k] = picked
+            begin(r, buf[r].at[k], rows[r].at[span(r, mine), chunk(k)], own_send.at[r, k], own_recv.at[r, k], peers[k - 1])
+
+    def spread(r, k):
+        here = rows[r].at[span(r, mine), chunk(k)]
+        if k:
+            arrive(here, own_recv.at[r, k])
+        for j in (1, 2):
+            begin(r, here, here, near_send.at[r, k, j], near_recv.at[r, k, j], near[j])
+        begin(r, here, here, pair_send.at[r, k, 0], pair_recv.at[r, k, 0], partner)
+
+    def forward(r, k):
+        for j in (1, 2):
+            place = span(r, block(j, core))
+            here = rows[r].at[place, chunk(k)]
+            arrive(here, near_recv.at[r, k, j])
+            part = rows[r].at[place, wings(k, j)]
+            begin(r, part, part, half_send.at[r, k, j], half_recv.at[r, k, j], near[3 - j])
+            begin(r, here, here, pair_send.at[r, k, j], pair_recv.at[r, k, j], partner)
+
+    def corner(r, k):
+        place = span(r, block(3, core))
+        for j in (1, 2):
+            arrive(rows[r].at[place, wings(k, j)], half_recv.at[r, k, j])
+        here = rows[r].at[place, chunk(k)]
+        begin(r, here, here, pair_send.at[r, k, 3], pair_recv.at[r, k, 3], partner)
+
+    def gathered(r, k):
+        for j in range(chips):
+            arrive(rows[r].at[span(r, block(j, 1 - core)), chunk(k)], pair_recv.at[r, k, j])
+        if r == 0:
+            loads[k][0].wait()
+            loads[k][1].wait()
+
+    def share_sums():
+        for k in range(1, experts):
+            begin("sums", sums, sums_in.at[k], sum_send.at[k], sum_recv.at[k], peers[k - 1])
+
+    def share_inverse():
+        total = sums[...]
+        for k in range(1, experts):
+            arrive(sums_in.at[k], sum_recv.at[k])
+            total = total + sums_in[k]
+        value = lax.rsqrt(total * (1.0 / features) + epsilon)[0:1, :]
+        column = jnp.sum(jnp.where(onehot[0] > 0.5, value, 0.0), axis=1, keepdims=True)
+        row = as_row(column, inverse_out.shape[1])
+        inverse_out[...] = jnp.broadcast_to(row, inverse_out.shape)
+        inverse_in[mine] = jnp.broadcast_to(row, inverse_out.shape)
+        for n, device in enumerate(plane):
+            begin("sums", inverse_out, inverse_in.at[mine], inv_send.at[n], inv_recv.at[mine], device)
+
+    def take_inverse():
+        for j in range(chips):
+            for which in range(2):
+                if j or which:
+                    index = block(j, mixed(core, which))
+                    arrive(inverse_in.at[index], inv_recv.at[index])
+        for b in range(chips * 2):
+            row = inverse_in[b][0:1, :]
+            column = jnp.sum(jnp.where(eye_of(cap, row.shape[1]), row, 0.0), axis=1, keepdims=True)
+            column = jnp.broadcast_to(column, (cap, 128))
+            base = 0
+            for r, count in enumerate(cuts):
+                inverse[r][b * count:(b + 1) * count, :] = column[base:base + count, :]
+                base += count
+
+    def activate(r, at, g, u):
+        by = inverse[r][:, 0:1]
+        g = g * by
+        u = u * by
+        hidden[r][:, at] = (g / (1.0 + jnp.exp(-g)) * u).astype(jnp.bfloat16)
+
+    tile = 512
+    body = inner // tile * tile
+
+    def up_tile(k):
+        def one(at):
+            g = times_transposed(rows_a[:, chunk(k)], wg[at, chunk(k)])
+            u = times_transposed(rows_a[:, chunk(k)], wu[at, chunk(k)])
+            if k:
+                g = g + acc_g[:, at]
+                u = u + acc_u[:, at]
+            if k == experts - 1:
+                activate(0, at, g, u)
+            else:
+                acc_g[:, at] = g
+                acc_u[:, at] = u
+        return one
+
+    def expand_first(k):
+        gathered(0, k)
+        if k == experts - 1:
+            take_inverse()
+        if body:
+            tiles(body, up_tile(k), tile)
+
+    def expand_rest(k):
+        if inner > body:
+            up_tile(k)(pl.ds(body, inner - body))
+
+    def whole_tile(at):
+        rest = pl.ds(width, (experts - 1) * width)
+        g = times_transposed(rows_b[:, rest], wg[at, rest]) + part_g[:, at]
+        u = times_transposed(rows_b[:, rest], wu[at, rest]) + part_u[:, at]
+        activate(1, at, g, u)
+
+    def expand_part():
+        gathered(1, 0)
+
+        def one(at):
+            part_g[:, at] = times_transposed(rows_b[:, chunk(0)], wg[at, chunk(0)])
+            part_u[:, at] = times_transposed(rows_b[:, chunk(0)], wu[at, chunk(0)])
+
+        tiles(inner, one, tile)
+
+    def multiply(r, k):
+        if r == 0:
+            downs[k].wait()
+        rows[r][:, chunk(k)] = jnp.dot(
+            hidden[r][...], wd[k], preferred_element_type=jnp.float32
+        ).astype(jnp.bfloat16)
+        half = chips * cuts[r]
+        there = pl.ds(pl.multiple_of((1 - core) * half, half), half)
+        begin("back", rows[r].at[there, chunk(k)], pair_in[r].at[k], swap_send.at[r, k], swap_recv.at[r, k], partner)
+
+    def paired(r, k, j, way):
+        inside = pl.ds((way - 1) * wing, wing)
+        return f32(rows[r][span(r, block(j, core)), wings(k, way)]) + f32(pair_in[r][k, span(r, mixed(chip, j)), inside])
+
+    def merge(r, k):
+        arrive(pair_in[r].at[k], swap_recv.at[r, k])
+        for way in (1, 2):
+            for slot, j in ((1, 3), (0, way)):
+                here = (span(r, block(j, core)), wings(k, way))
+                rows[r][here] = paired(r, k, j, way).astype(jnp.bfloat16)
+                begin(
+                    "back", rows[r].at[here], near_in[r].at[k, way - 1, slot],
+                    one_send.at[r, k, way - 1, slot], one_recv.at[r, k, way - 1, slot], near[way],
+                )
+
+    def relay(r, k):
+        for way in (1, 2):
+            arrive(near_in[r].at[k, way - 1, 1], one_recv.at[r, k, way - 1, 1])
+            j = 3 - way
+            value = paired(r, k, j, way) + f32(near_in[r][k, way - 1, 1])
+            here = (span(r, block(j, core)), wings(k, way))
+            rows[r][here] = value.astype(jnp.bfloat16)
+            begin(
+                "back", rows[r].at[here], far_in[r].at[k, way - 1],
+                two_send.at[r, k, way - 1], two_recv.at[r, k, way - 1], near[j],
+            )
+
+    def finish(r, k):
+        for way in (1, 2):
+            arrive(near_in[r].at[k, way - 1, 0], one_recv.at[r, k, way - 1, 0])
+            arrive(far_in[r].at[k, way - 1], two_recv.at[r, k, way - 1])
+            value = paired(r, k, 0, way) + f32(near_in[r][k, way - 1, 0]) + f32(far_in[r][k, way - 1])
+            inside = pl.ds((way - 1) * wing, wing)
+            if k == 0:
+                back[r][0, :, inside] = value.astype(jnp.bfloat16)
+            else:
+                final[r][k, :, inside] = value.astype(jnp.bfloat16)
+        if k:
+            begin("back", final[r].at[k], back[r].at[k], ret_send.at[r, k], ret_recv.at[r, k], peers[k - 1])
+
+    def combine(r):
+        for k in range(1, experts):
+            arrive(back[r].at[k], ret_recv.at[r, k])
+        given = back[r][...].reshape(experts * cuts[r], width)
+        value = f32(residual[...]) if r == 0 else summed[...]
+        for which in range(2):
+            value = value + lax.dot_general(
+                weigh[r][which], given, (((0,), (0,)), ((), ())), preferred_element_type=jnp.float32
+            )
+        if r == 0:
+            summed[...] = value
+        else:
+            out[...] = value.astype(jnp.bfloat16)
+
+    prepare()
+    share_sums()
+    route(0, 0)
+    spread(0, 0)
+    for k in range(1, experts):
+        route(0, k)
+    route(1, 0)
+    spread(1, 0)
+
+    forward(0, 0)
+    spread(0, 1)
+    corner(0, 0)
+    forward(1, 0)
+    expand_first(0)
+    forward(0, 1)
+    spread(0, 2)
+    corner(1, 0)
+    expand_rest(0)
+    for k in range(1, experts):
+        route(1, k)
+    expand_part()
+    corner(0, 1)
+    forward(0, 2)
+    spread(0, 3)
+    share_inverse()
+    expand_first(1)
+    corner(0, 2)
+    forward(0, 3)
+    spread(1, 1)
+    expand_rest(1)
+    expand_first(2)
+    corner(0, 3)
+    forward(1, 1)
+    spread(1, 2)
+    expand_rest(2)
+    expand_first(3)
+    corner(1, 1)
+    forward(1, 2)
+    spread(1, 3)
+    expand_rest(3)
+    settle(0)
+    multiply(0, 3)
+    corner(1, 2)
+    forward(1, 3)
+    multiply(0, 2)
+    merge(0, 3)
+    multiply(0, 1)
+    merge(0, 2)
+    multiply(0, 0)
+    corner(1, 3)
+    merge(0, 1)
+    relay(0, 3)
+    for k in range(1, experts):
+        gathered(1, k)
+    merge(0, 0)
+    cuts_at = [pl.ds(at, min(tile, inner - at)) for at in range(0, inner, tile)]
+    between = [
+        ((relay, 2), (finish, 3)),
+        ((relay, 1), (relay, 0), (finish, 2)),
+        ((finish, 1), (finish, 0)),
+    ]
+    for n, at in enumerate(cuts_at):
+        whole_tile(at)
+        for action, k in between[n] if n < len(between) else ():
+            action(0, k)
+    for group in between[len(cuts_at):]:
+        for action, k in group:
+            action(0, k)
+    settle(1)
+    multiply(1, 3)
+    multiply(1, 2)
+    merge(1, 3)
+    multiply(1, 1)
+    merge(1, 2)
+    multiply(1, 0)
+    merge(1, 1)
+    relay(1, 3)
+    merge(1, 0)
+    relay(1, 2)
+    finish(1, 3)
+    relay(1, 1)
+    combine(0)
+    finish(1, 2)
+    relay(1, 0)
+    finish(1, 1)
+    finish(1, 0)
+    combine(1)
+    settle("back")
+    settle("sums")
+
+
+def run_square_experts(experts, cap, residual, ids, scale, gain, gate, up, down):
+    tokens, width = residual.shape
+    inner = gate.shape[1]
+    chips = 4
+    first = cap // 16 * 3 // 5 * 16
+    cuts = (first, cap - first)
+    bf16, f32 = jnp.bfloat16, jnp.float32
+    dma = pltpu.SemaphoreType.DMA
+    vmem = pl.BlockSpec(memory_space=pltpu.VMEM)
+    hbm = pl.BlockSpec(memory_space=pl.ANY)
+
+    def both(shape, dtype=bf16):
+        return [pltpu.VMEM(shape(count), dtype) for count in cuts]
+
+    return pl.pallas_call(
+        functools.partial(square_experts_kernel, experts, cuts),
+        out_shape=jax.ShapeDtypeStruct((tokens, width), bf16),
+        in_specs=[vmem, vmem, vmem, vmem, hbm, hbm, hbm],
+        out_specs=vmem,
+        scratch_shapes=[
+            pltpu.VMEM((experts, cap, tokens), bf16),
+            *both(lambda n: (2, experts * n, tokens)),
+            pltpu.VMEM((tokens, width), bf16),
+            *both(lambda n: (experts, n, width)),
+            *both(lambda n: (chips * 2 * n, experts * width)),
+            pltpu.VMEM((inner, experts * width), bf16),
+            pltpu.VMEM((inner, experts * width), bf16),
+            pltpu.VMEM((experts, inner, width), bf16),
+            pltpu.VMEM((chips * 2 * cuts[0], inner), f32),
+            pltpu.VMEM((chips * 2 * cuts[0], inner), f32),
+            pltpu.VMEM((chips * 2 * cuts[1], inner), f32),
+            pltpu.VMEM((chips * 2 * cuts[1], inner), f32),
+            *both(lambda n: (chips * 2 * n, inner)),
+            *both(lambda n: (experts, chips * n, width)),
+            *both(lambda n: (experts, 2, 2, n, width // 2)),
+            *both(lambda n: (experts, 2, n, width // 2)),
+            *both(lambda n: (experts, n, width)),
+            *both(lambda n: (experts, n, width)),
+            pltpu.VMEM((tokens, width), f32),
+            pltpu.VMEM((8, tokens), f32),
+            pltpu.VMEM((experts, 8, tokens), f32),
+            pltpu.VMEM((8, 128), f32),
+            pltpu.VMEM((chips * 2, 8, 128), f32),
+            *both(lambda n: (chips * 2 * n, 128), f32),
+            dma((3, experts)),
+            dma((2, experts)),
+            dma((2, experts)),
+            dma((2, experts, 3)),
+            dma((2, experts, 3)),
+            dma((2, experts, 3)),
+            dma((2, experts, 3)),
+            dma((2, experts, 4)),
+            dma((2, experts, 4)),
+            dma((2, experts)),
+            dma((2, experts)),
+            dma((2, experts, 2, 2)),
+            dma((2, experts, 2, 2)),
+            dma((2, experts, 2)),
+            dma((2, experts, 2)),
+            dma((2, experts)),
+            dma((2, experts)),
+            dma((experts,)),
+            dma((experts,)),
+            dma((chips * 2 - 1,)),
+            dma((chips * 2,)),
+        ],
+        compiler_params=pltpu.CompilerParams(
+            collective_id=3, has_side_effects=True, vmem_limit_bytes=67043328
+        ),
+        name="square_experts",
+    )(residual, ids, scale, gain, gate, up, down)
+
+
 def attend(query_heads, key_rows, value_rows, query_offset):
     head_count, row_count, head_width = query_heads.shape
     key_count = key_rows.shape[0]
@@ -482,6 +947,19 @@
     )
     capacity = min(row_count, 5 * row_count // (2 * expert_count))
     capacity = -(-capacity // 16) * 16
+    if chips == 4 and expert_count == 4:
+        residual = project(expert_count, attended, out_weight, hidden_in)
+        return run_square_experts(
+            expert_count,
+            capacity,
+            residual,
+            expert_ids.T,
+            gate_scale.T,
+            norm_gain.reshape(expert_count, 1, local_width),
+            gate_proj.transpose(0, 2, 1),
+            up_proj.transpose(0, 2, 1),
+            down_proj,
+        )
     flat_ids = jnp.bitwise_xor(expert_ids.reshape(row_count * 2), lax.axis_index("exp"))
     onehot = (
         flat_ids[:, None] == lax.broadcasted_iota(jnp.int32, (row_count * 2, expert_count), 1)

time: 145 us -> 126 us (0.87)
  Pallas kernels: 126 us -> 115 us
  other arithmetic: 3.37 us -> 0.1 us
  matrix products: 6.51 us -> 3.78 us
    pallas_call x1, Pallas kernels: 84.3 us -> 73.1 us  [run_square_experts(): pl.pallas_call(functools.partial(square_experts_kernel, experts, cuts), o...]
    dot_general x2 -> x0, matrix products: 2.75 us -> none  [the longest x1 1.57 us: local(): lax.dot_general(placing, returned, (((0,), (0,)), ((), ())), preferred_el...]
    convert_element_type x2 -> x0, other arithmetic: 1.83 us -> none  [the longest x1 1.83 us: local(): return combined.astype(jnp.bfloat16)]
    unnamed x13 -> x11, local copies, waits for them, and re-layouts: 4.24 us -> 4.56 us
where the time goes in v1:
time: 126 us
  Pallas kernels  115 us (91%)
  local copies, waits for them, and re-layouts  7.05 us (6%)
  matrix products  3.78 us (3%)
    pallas_call x1, Pallas kernels, run_square_experts(): pl.pallas_call(functools.partial(square_experts_kernel, experts, cuts), o...  73.1 us
    pallas_call x1, Pallas kernels, project(): pl.pallas_call(functools.partial(project_kernel, experts), out_shape=jax....  22.6 us
    pallas_call x1, Pallas kernels, gather_blocks(): pl.pallas_call(functools.partial(gather_kernel, chips), out_shape=(whole,...  19.2 us
    unnamed x11, local copies, waits for them, and re-layouts  4.56 us

profile of v1, /device:TPU:0, one launch (start us, length us, event | category | flops | bytes accessed | tf_op | source)
XLA Modules:
  0.0 126.0 jit_solution(8863720561303919120)
XLA Ops:
  0.0 0.0 copy-start.4
  0.0 0.1 iota_compare_fusion
  0.1 19.2 %gather_blocks.1 = (bf16[1024,512]{1,0:T(8,128)(2,1)}, bf16[1024,512]{1,0:T(8,128)(2,1)}) custom-call(bf16[128,512]{1,0:T(8,128)(2,1)} %k_ref.1, bf16[128,512]{1,0:T(8,128)(2,1)} %v_ref.1), custom_call_target="tpu_custom_call" | custom-call | tf_op jit(solution)/shard_map/gather_blocks/pallas_call | solution.py:113
  19.3 0.0 copy-start.3
  19.3 2.4 %copy.18 = bf16[1024,512]{0,1:T(8,128)(2,1)} copy(bf16[1024,512]{1,0:T(8,128)(2,1)} %get-tuple-element.8) | data formatting | bytes 2097152 | tf_op jit(solution)/shard_map/reshape | solution.py:904
  21.7 0.0 copy-done.4
  21.7 0.0 copy-done.3
  21.7 1.0 fusion.24
  22.8 0.4 fusion.4
  23.2 0.0 copy-start.2
  23.2 2.3 %fusion.3 = bf16[128,4,128]{0,2,1:T(8,128)(2,1)S(1)} fusion(bf16[1024,4,128]{0,2,1:T(8,128)(2,1)} %bitcast.71, f32[4,1024,128]{2,1,0:T(8,128)S(1)} %fusion.4, pred[128,1024]{0,1:T(8,128)(4,1)S(1)} %iota_compare_fusion, f32[128,4]{0,1:T(4,128)S(1)} %bitcast.76), kind=kOutput, calls=%fused_computation.6 | convolution fusion | flops 136971776 | bytes 3409920 | tf_op jit(solution)/shard_map/hqk,khd->hqd/dot_general | solution.py:914
  25.5 0.1 copy.19.att_ref
  25.6 0.0 copy-done.2
  25.7 0.0 copy-start
  25.7 2.2 %copy-done = bf16[512,4096]{1,0:T(8,128)(2,1)S(1)} copy-done((bf16[512,4096]{1,0:T(8,128)(2,1)S(1)}, bf16[512,4096]{1,0:T(8,128)(2,1)}, u32[]{:S(2)}) %copy-start) | copy-done | bytes 4194328
  27.8 22.6 %project_reduce.1.residual = bf16[128,1024]{1,0:T(8,128)(2,1)S(1)} custom-call(bf16[128,512]{1,0:T(8,128)(2,1)S(1)} %copy.19.att_ref, bf16[512,4096]{1,0:T(8,128)(2,1)S(1)} %copy-done, bf16[128,1024]{1,0:T(8,128)(2,1)S(1)} %copy-done.2), custom_call_target="tpu_custom_call" | custom-call | tf_op jit(solution)/shard_map/project_reduce/pallas_call | solution.py:180
  50.5 0.0 copy-start.1
  50.5 0.7 copy-done.1
  51.2 73.1 %square_experts.1 = bf16[128,1024]{1,0:T(8,128)(2,1)} custom-call(bf16[128,1024]{1,0:T(8,128)(2,1)} %copy-done.1, s32[2,128]{1,0:T(2,128)} %bitcast.74, f32[2,128]{1,0:T(2,128)} %bitcast.75, f32[4,1,1024]{2,1,0:T(1,128)} %bitcast.73, bf16[1,1376,4096]{2,1,0:T(8,128)(2,1)} %bitcast.69, bf16[1,1376,4096]{2,1,0:T(8,128)(2,1)} %bitcast.70, ...), custom_call_target="tpu_custom_call" | custom-call | tf_op jit(solution)/shard_map/square_experts/pallas_call | solution.py:841
  124.3 1.7 %copy.43 = bf16[128,1024]{1,0:T(8,128)(2,1)} copy(bf16[128,1024]{1,0:T(8,128)(2,1)} %square_experts.1) | data formatting | bytes 524288
  (1 shorter events, 0.0 us)
Async XLA Ops:
  0.0 21.7 %copy-start.4 = (bf16[128,512]{1,0:T(8,128)(2,1)S(1)}, bf16[128,512]{1,0:T(8,128)(2,1)}, u32[]{:S(2)}) copy-start(bf16[128,512]{1,0:T(8,128)(2,1)} %param.12) | copy-start | bytes 393220
  19.3 2.4 %copy-start.3 = (bf16[1024,512]{1,0:T(8,128)(2,1)S(1)}, bf16[1024,512]{1,0:T(8,128)(2,1)}, u32[]{:S(2)}) copy-start(bf16[1024,512]{1,0:T(8,128)(2,1)} %get-tuple-element.7) | copy-start | bytes 3145732
  23.2 2.4 %copy-start.2 = (bf16[128,1024]{1,0:T(8,128)(2,1)S(1)}, bf16[128,1024]{1,0:T(8,128)(2,1)}, u32[]{:S(2)}) copy-start(bf16[128,1024]{1,0:T(8,128)(2,1)} %hidden_ref.1) | copy-start | bytes 786436
  25.7 2.2 %copy-start = (bf16[512,4096]{1,0:T(8,128)(2,1)S(1)}, bf16[512,4096]{1,0:T(8,128)(2,1)}, u32[]{:S(2)}) copy-start(bf16[512,4096]{1,0:T(8,128)(2,1)} %weight_ref.1) | copy-start | bytes 12582916
  50.5 0.7 copy-start.1

commit v2 on v1

--- a/solution.py
+++ b/solution.py
@@ -897,6 +897,210 @@
     )(residual, ids, scale, gain, gate, up, down)
 
 
+def attend_kernel(
+    experts, query_hbm, key_hbm, value_hbm, hidden_hbm, weight_hbm, out,
+    query, hidden, keys, values, share, own_weight, walls, att,
+    load_sem, near_send, near_recv, half_send, half_recv, pair_send, pair_recv,
+    share_send, share_recv, att_send, att_recv,
+):
+    chips = 4
+    ctx, exp = lax.axis_index("ctx"), lax.axis_index("exp")
+    chip, core = ctx // 2, ctx % 2
+    tokens, depth = query.shape
+    width = hidden.shape[1]
+    heads = depth // HEAD_DIM
+    strip = share.shape[1]
+    partner = (chip * 2 + 1 - core, exp)
+    near = {j: (mixed(chip, j) * 2 + core, exp) for j in (1, 2)}
+    peers = [(ctx, mixed(exp, k)) for k in range(1, experts)]
+    arrays = [keys, values] + [walls.at[k] for k in range(experts - 1)]
+
+    def columns(k):
+        return pl.ds(pl.multiple_of(mixed(exp, k) * width, width), width)
+
+    mine = pl.ds(pl.multiple_of(ctx * strip, strip), strip)
+    loads = [
+        pltpu.make_async_copy(weight_hbm.at[mine, columns(k)], share.at[k - 1], load_sem.at[k])
+        for k in range(1, experts)
+    ]
+    first_rows = pl.ds(pl.multiple_of(ctx * tokens, tokens), tokens)
+    inputs = [
+        pltpu.make_async_copy(src, dst, load_sem.at[experts + n])
+        for n, (src, dst) in enumerate((
+            (key_hbm, keys.at[first_rows, :]), (value_hbm, values.at[first_rows, :]), (query_hbm, query), (hidden_hbm, hidden)
+        ))
+    ]
+    for load in inputs:
+        load.start()
+    own_load = pltpu.make_async_copy(weight_hbm.at[:, columns(0)], own_weight, load_sem.at[0])
+    for load in loads:
+        load.start()
+    own_load.start()
+    greet([partner, near[1], near[2]] + peers)
+
+    sent = []
+
+    def begin(src, dst, send_sem, recv_sem, device):
+        copy = remote(src, dst, send_sem, recv_sem, device)
+        copy.start()
+        sent.append(copy)
+
+    def arrive(view, recv_sem):
+        remote(view, view, att_send.at[0], recv_sem, partner).wait_recv()
+
+    def block(i, j, which):
+        size = tokens if i < 2 else strip
+        owner = mixed(chip, j) * 2 + which
+        return pl.ds(pl.multiple_of(owner * size, size), size)
+
+    def half(i, j):
+        size = arrays[i].shape[1] // 2
+        return pl.ds((j - 1) * size, size)
+
+    def spread(i):
+        here = arrays[i].at[block(i, 0, core), :]
+        for j in (1, 2):
+            begin(here, here, near_send.at[i, j - 1], near_recv.at[i, j - 1], near[j])
+        begin(here, here, pair_send.at[i, 0], pair_recv.at[i, 0], partner)
+
+    def forward(i):
+        for j in (1, 2):
+            here = arrays[i].at[block(i, j, core), :]
+            arrive(here, near_recv.at[i, j - 1])
+            part = arrays[i].at[block(i, j, core), half(i, j)]
+            begin(part, part, half_send.at[i, j - 1], half_recv.at[i, j - 1], near[3 - j])
+            begin(here, here, pair_send.at[i, j], pair_recv.at[i, j], partner)
+
+    def corner(i):
+        for j in (1, 2):
+            arrive(arrays[i].at[block(i, 3, core), half(i, j)], half_recv.at[i, j - 1])
+        here = arrays[i].at[block(i, 3, core), :]
+        begin(here, here, pair_send.at[i, 3], pair_recv.at[i, 3], partner)
+
+    def passed(i, j):
+        arrive(arrays[i].at[block(i, j, 1 - core), :], pair_recv.at[i, j])
+
+    state = [None] * heads
+
+    def attend_chip(j):
+        count = 2 * tokens
+        start = mixed(chip, j) * count
+        rows = pl.ds(pl.multiple_of(start, count), count)
+        query_pos = ctx * tokens + lax.broadcasted_iota(jnp.int32, (tokens, count), 0)
+        key_pos = start + lax.broadcasted_iota(jnp.int32, (tokens, count), 1)
+        visible = key_pos <= query_pos
+        for h in range(heads):
+            cols = pl.ds(h * HEAD_DIM, HEAD_DIM)
+            scores = times_transposed(query[:, cols], keys[rows, cols]) * HEAD_DIM ** (-0.5)
+            scores = jnp.where(visible, scores, masked_score)
+            top = jnp.max(scores, axis=1, keepdims=True)
+            if state[h] is not None:
+                top = jnp.maximum(top, state[h][0])
+            weights = jnp.where(visible, jnp.exp(scores - top), 0.0)
+            total = jnp.sum(weights, axis=1, keepdims=True)
+            part = jnp.dot(weights.astype(jnp.bfloat16), values[rows, cols], preferred_element_type=jnp.float32)
+            if state[h] is not None:
+                fade = jnp.exp(state[h][0] - top)
+                total = total + state[h][1] * fade
+                part = part + state[h][2] * fade
+            state[h] = (top, total, part)
+
+    inputs[0].wait()
+    spread(0)
+    inputs[1].wait()
+    spread(1)
+    for k in range(1, experts):
+        loads[k - 1].wait()
+        begin(share.at[k - 1], walls.at[k - 1, mine, :], share_send.at[k], share_recv.at[k], peers[k - 1])
+
+    def take_share(k):
+        arrive(walls.at[k - 1, mine, :], share_recv.at[k])
+        spread(k + 1)
+
+    passed(0, 0)
+    passed(1, 0)
+    inputs[2].wait()
+    attend_chip(0)
+    forward(0)
+    forward(1)
+    take_share(1)
+    for j in (1, 2):
+        passed(0, j)
+        passed(1, j)
+        attend_chip(j)
+    take_share(2)
+    corner(0)
+    corner(1)
+    passed(0, 3)
+    passed(1, 3)
+    attend_chip(3)
+    for h in range(heads):
+        att[0, :, h * HEAD_DIM:(h + 1) * HEAD_DIM] = (state[h][2] / state[h][1]).astype(jnp.bfloat16)
+    for k in range(1, experts):
+        begin(att.at[0], att.at[k], att_send.at[k], att_recv.at[k], peers[k - 1])
+    forward(2)
+    take_share(3)
+    forward(3)
+    corner(2)
+    forward(4)
+    inputs[3].wait()
+    total = hidden[...].astype(jnp.float32)
+    own_load.wait()
+    total = total + jnp.dot(att[0], own_weight[...], preferred_element_type=jnp.float32)
+    for k in range(2, experts):
+        corner(k + 1)
+    for k in range(1, experts):
+        for j in range(chips):
+            passed(k + 1, j)
+        arrive(att.at[k], att_recv.at[k])
+        total = total + jnp.dot(att[k], walls[k - 1], preferred_element_type=jnp.float32)
+    out[...] = total.astype(jnp.bfloat16)
+    for copy in sent:
+        copy.wait_send()
+
+
+def attend_project(experts, query, key, value, hidden, weight):
+    tokens, width = hidden.shape
+    depth = query.shape[1]
+    chips = 4
+    strip = depth // (chips * 2)
+    bf16 = jnp.bfloat16
+    dma = pltpu.SemaphoreType.DMA
+    vmem = pl.BlockSpec(memory_space=pltpu.VMEM)
+    hbm = pl.BlockSpec(memory_space=pl.ANY)
+    return pl.pallas_call(
+        functools.partial(attend_kernel, experts),
+        out_shape=jax.ShapeDtypeStruct((tokens, width), bf16),
+        in_specs=[hbm] * 5,
+        out_specs=vmem,
+        scratch_shapes=[
+            pltpu.VMEM((tokens, depth), bf16),
+            pltpu.VMEM((tokens, width), bf16),
+            pltpu.VMEM((chips * 2 * tokens, depth), bf16),
+            pltpu.VMEM((chips * 2 * tokens, depth), bf16),
+            pltpu.VMEM((experts - 1, strip, width), bf16),
+            pltpu.VMEM((depth, width), bf16),
+            pltpu.VMEM((experts - 1, depth, width), bf16),
+            pltpu.VMEM((experts, tokens, depth), bf16),
+            dma((experts + 4,)),
+            dma((experts + 1, 2)),
+            dma((experts + 1, 2)),
+            dma((experts + 1, 2)),
+            dma((experts + 1, 2)),
+            dma((experts + 1, 4)),
+            dma((experts + 1, 4)),
+            dma((experts,)),
+            dma((experts,)),
+            dma((experts,)),
+            dma((experts,)),
+        ],
+        compiler_params=pltpu.CompilerParams(
+            collective_id=4, has_side_effects=True, vmem_limit_bytes=67043328
+        ),
+        name="attend_project",
+    )(query, key, value, hidden, weight)
+
+
 def attend(query_heads, key_rows, value_rows, query_offset):
     head_count, row_count, head_width = query_heads.shape
     key_count = key_rows.shape[0]
@@ -937,18 +1141,12 @@
     head_count = query_vectors.shape[1] // HEAD_DIM
     chips = lax.axis_size("ctx") // 2
     expert_count = lax.axis_size("exp")
-    query_heads = query_vectors.reshape(row_count, head_count, HEAD_DIM).transpose(1, 0, 2)
-    keys, values = gather_blocks(chips, key_vectors, value_vectors)
-    attended = (
-        attend(query_heads, keys, values, lax.axis_index("ctx") * row_count)
-        .transpose(1, 0, 2)
-        .reshape(row_count, head_count * HEAD_DIM)
-        .astype(jnp.bfloat16)
-    )
     capacity = min(row_count, 5 * row_count // (2 * expert_count))
     capacity = -(-capacity // 16) * 16
     if chips == 4 and expert_count == 4:
-        residual = project(expert_count, attended, out_weight, hidden_in)
+        residual = attend_project(
+            expert_count, query_vectors, key_vectors, value_vectors, hidden_in, out_weight
+        )
         return run_square_experts(
             expert_count,
             capacity,
@@ -960,6 +1158,14 @@
             up_proj.transpose(0, 2, 1),
             down_proj,
         )
+    query_heads = query_vectors.reshape(row_count, head_count, HEAD_DIM).transpose(1, 0, 2)
+    keys, values = gather_blocks(chips, key_vectors, value_vectors)
+    attended = (
+        attend(query_heads, keys, values, lax.axis_index("ctx") * row_count)
+        .transpose(1, 0, 2)
+        .reshape(row_count, head_count * HEAD_DIM)
+        .astype(jnp.bfloat16)
+    )
     flat_ids = jnp.bitwise_xor(expert_ids.reshape(row_count * 2), lax.axis_index("exp"))
     onehot = (
         flat_ids[:, None] == lax.broadcasted_iota(jnp.int32, (row_count * 2, expert_count), 1)

time: 126 us -> 108 us (0.86)
  Pallas kernels: 115 us -> 107 us
  local copies, waits for them, and re-layouts: 7.05 us -> 1.67 us
  matrix products: 3.78 us -> 0 us
    pallas_call x2 -> x1, Pallas kernels: 41.9 us -> 32 us  [attend_project(): pl.pallas_call(functools.partial(attend_kernel, experts), out_shape=jax.S...]
    unnamed x11 -> x1, local copies, waits for them, and re-layouts: 4.56 us -> 1.67 us
    dot_general x2 -> x0, matrix products: 2.75 us -> none  [the longest x1 2.31 us: attend(): jnp.einsum('hqk,khd->hqd', weights.astype(jnp.bfloat16), value_split, pre...]
    reshape x1 -> x0, local copies, waits for them, and re-layouts: 2.37 us -> none  [attend(): value_split = value_rows.reshape(key_count, head_count, head_width)]
    pallas_call x1, Pallas kernels: 73.1 us -> 74.6 us  [run_square_experts(): pl.pallas_call(functools.partial(square_experts_kernel, experts, cuts), o...]
where the time goes in v2:
time: 108 us
  Pallas kernels  107 us (99%)
  local copies, waits for them, and re-layouts  1.67 us (2%)
    pallas_call x1, Pallas kernels, run_square_experts(): pl.pallas_call(functools.partial(square_experts_kernel, experts, cuts), o...  74.6 us
    pallas_call x1, Pallas kernels, attend_project(): pl.pallas_call(functools.partial(attend_kernel, experts), out_shape=jax.S...  32 us

profile of v2, /device:TPU:0, one launch (start us, length us, event | category | flops | bytes accessed | tf_op | source)
XLA Modules:
  0.0 108.3 jit_solution(619930468510239793)
XLA Ops:
  0.0 32.0 %attend_project.1.residual = bf16[128,1024]{1,0:T(8,128)(2,1)} custom-call(bf16[128,512]{1,0:T(8,128)(2,1)} %query_hbm.1, bf16[128,512]{1,0:T(8,128)(2,1)} %key_hbm.1, bf16[128,512]{1,0:T(8,128)(2,1)} %value_hbm.1, bf16[128,1024]{1,0:T(8,128)(2,1)} %hidden_hbm.1, bf16[512,4096]{1,0:T(8,128)(2,1)} %weight_hbm.1), custom_call_target="tpu_custom_call" | custom-call | tf_op jit(solution)/shard_map/attend_project/pallas_call | solution.py:1071
  32.0 74.6 %square_experts.1 = bf16[128,1024]{1,0:T(8,128)(2,1)} custom-call(bf16[128,1024]{1,0:T(8,128)(2,1)} %attend_project.1.residual, s32[2,128]{1,0:T(2,128)} %bitcast.8, f32[2,128]{1,0:T(2,128)} %bitcast.9, f32[4,1,1024]{2,1,0:T(1,128)} %bitcast.7, bf16[1,1376,4096]{2,1,0:T(8,128)(2,1)} %bitcast.5, bf16[1,1376,4096]{2,1,0:T(8,128)(2,1)} %bitcast.6, ...), custom_call_target="tpu_custom_call" | custom-call | tf_op jit(solution)/shard_map/square_experts/pallas_call | solution.py:841
  106.6 1.7 %copy.13 = bf16[128,1024]{1,0:T(8,128)(2,1)} copy(bf16[128,1024]{1,0:T(8,128)(2,1)} %square_experts.1) | data formatting | bytes 524288

commit v3 on v2

--- a/solution.py
+++ b/solution.py
@@ -432,6 +432,16 @@
     )(buffer, gain, gate, up, down)
 
 
+def announce(devices):
+    barrier = pltpu.get_barrier_semaphore()
+    for device in devices:
+        pl.semaphore_signal(barrier, inc=1, device_id=device, device_id_type=MESH)
+
+
+def admit(devices):
+    pl.semaphore_wait(pltpu.get_barrier_semaphore(), len(devices))
+
+
 def eye_of(rows, columns):
     return lax.broadcasted_iota(jnp.int32, (rows, columns), 0) == lax.broadcasted_iota(jnp.int32, (rows, columns), 1)
 
@@ -537,8 +547,8 @@
             copy.wait_send()
         started[group].clear()
 
+    announce(plane + peers)
     routed(ids, scale, onehot, weigh, cuts, experts, exp)
-    greet(plane + peers)
 
     def prepare():
         x = f32(residual[...])
@@ -555,6 +565,9 @@
             rows[r][span(r, mine), chunk(0)] = picked
         else:
             buf[r][k] = picked
+
+    def deliver(r):
+        for k in range(1, experts):
             begin(r, buf[r].at[k], rows[r].at[span(r, mine), chunk(k)], own_send.at[r, k], own_recv.at[r, k], peers[k - 1])
 
     def spread(r, k):
@@ -734,12 +747,13 @@
             out[...] = value.astype(jnp.bfloat16)
 
     prepare()
-    share_sums()
-    route(0, 0)
-    spread(0, 0)
-    for k in range(1, experts):
+    for k in range(experts):
         route(0, k)
     route(1, 0)
+    admit(plane + peers)
+    share_sums()
+    spread(0, 0)
+    deliver(0)
     spread(1, 0)
 
     forward(0, 0)
@@ -753,6 +767,7 @@
     expand_rest(0)
     for k in range(1, experts):
         route(1, k)
+    deliver(1)
     expand_part()
     corner(0, 1)
     forward(0, 2)
@@ -760,9 +775,9 @@
     share_inverse()
     expand_first(1)
     corner(0, 2)
+    expand_rest(1)
     forward(0, 3)
     spread(1, 1)
-    expand_rest(1)
     expand_first(2)
     corner(0, 3)
     forward(1, 1)
@@ -781,8 +796,8 @@
     merge(0, 3)
     multiply(0, 1)
     merge(0, 2)
+    corner(1, 3)
     multiply(0, 0)
-    corner(1, 3)
     merge(0, 1)
     relay(0, 3)
     for k in range(1, experts):
@@ -790,9 +805,9 @@
     merge(0, 0)
     cuts_at = [pl.ds(at, min(tile, inner - at)) for at in range(0, inner, tile)]
     between = [
-        ((relay, 2), (finish, 3)),
-        ((relay, 1), (relay, 0), (finish, 2)),
-        ((finish, 1), (finish, 0)),
+        ((relay, 2),),
+        ((relay, 1), (finish, 3)),
+        ((relay, 0), (finish, 2)),
     ]
     for n, at in enumerate(cuts_at):
         whole_tile(at)
@@ -803,8 +818,10 @@
             action(0, k)
     settle(1)
     multiply(1, 3)
+    finish(0, 1)
     multiply(1, 2)
     merge(1, 3)
+    finish(0, 0)
     multiply(1, 1)
     merge(1, 2)
     multiply(1, 0)

time: 108 us -> 105 us (0.972)
  Pallas kernels: 107 us -> 104 us
    pallas_call x1, Pallas kernels: 74.6 us -> 71.6 us  [run_square_experts(): pl.pallas_call(functools.partial(square_experts_kernel, experts, cuts), o...]
where the time goes in v3:
time: 105 us
  Pallas kernels  104 us (99%)
  local copies, waits for them, and re-layouts  1.67 us (2%)
    pallas_call x1, Pallas kernels, run_square_experts(): pl.pallas_call(functools.partial(square_experts_kernel, experts, cuts), o...  71.6 us
    pallas_call x1, Pallas kernels, attend_project(): pl.pallas_call(functools.partial(attend_kernel, experts), out_shape=jax.S...  32 us

profile of v3, /device:TPU:0, one launch (start us, length us, event | category | flops | bytes accessed | tf_op | source)
XLA Modules:
  0.0 105.3 jit_solution(6098473335483884798)
XLA Ops:
  0.0 32.0 %attend_project.1.residual = bf16[128,1024]{1,0:T(8,128)(2,1)} custom-call(bf16[128,512]{1,0:T(8,128)(2,1)} %query_hbm.1, bf16[128,512]{1,0:T(8,128)(2,1)} %key_hbm.1, bf16[128,512]{1,0:T(8,128)(2,1)} %value_hbm.1, bf16[128,1024]{1,0:T(8,128)(2,1)} %hidden_hbm.1, bf16[512,4096]{1,0:T(8,128)(2,1)} %weight_hbm.1), custom_call_target="tpu_custom_call" | custom-call | tf_op jit(solution)/shard_map/attend_project/pallas_call | solution.py:1088
  32.0 71.6 %square_experts.1 = bf16[128,1024]{1,0:T(8,128)(2,1)} custom-call(bf16[128,1024]{1,0:T(8,128)(2,1)} %attend_project.1.residual, s32[2,128]{1,0:T(2,128)} %bitcast.8, f32[2,128]{1,0:T(2,128)} %bitcast.9, f32[4,1,1024]{2,1,0:T(1,128)} %bitcast.7, bf16[1,1376,4096]{2,1,0:T(8,128)(2,1)} %bitcast.5, bf16[1,1376,4096]{2,1,0:T(8,128)(2,1)} %bitcast.6, ...), custom_call_target="tpu_custom_call" | custom-call | tf_op jit(solution)/shard_map/square_experts/pallas_call | solution.py:858
  103.6 1.7 %copy.13 = bf16[128,1024]{1,0:T(8,128)(2,1)} copy(bf16[128,1024]{1,0:T(8,128)(2,1)} %square_experts.1) | data formatting | bytes 524288
